TPU v7x, 256 devices: a whole 4x4x8 slice. The times are simulated.
256 devices in a mesh: section: 8 (over y, z_hi), dp: 32 (over z_lo, x, core).
Axes of the slice: x: 4, y: 4, z: 8 (z_hi: 2, z_lo: 4; z = z_hi * 4 + z_lo), core: 2. Of those that a mesh axis runs over, the one named last changes fastest.
Arguments:
- residuals: float32 [32, 1024, 4096], P('section', 'dp'), may hold values from -100 to 100, as said below
- owners: int32 [256], replicated, may hold values from 0 to 255, each once
Outputs:
- harvest: bfloat16 [1024, 32, 4096], P(('section', 'dp'))
Inputs may be any that keep to these rules, and one draw needn't show every extreme that they name: `owners`: a permutation of the block numbers. `residuals`: real-valued activations.
All inputs are finite; a program needn't handle non-finite values.
Results may differ from a plain program's by a relative error of at most 0.0004.
Values may be sent and summed in bfloat16 or wider, within the bound.
A program may use at most 64 MiB of HBM per device.

v0:
```python
import jax
import jax.numpy as jnp
from jax import lax
from jax.sharding import Mesh
from jax.sharding import PartitionSpec as P

DP = ("dp_0", "dp_1", "dp_2")
DP_SECTION = ("dp_0", "dp_1", "dp_2", "section")
SECTION_DP = ("section", "dp_0", "dp_1", "dp_2")


def sent_to_all(array, axis):
    copies = jnp.broadcast_to(array, (lax.axis_size(axis), *array.shape))
    return lax.all_to_all(copies, axis, split_axis=0, concat_axis=0, tiled=True)


def over_copies(array, axis):
    return sent_to_all(array, axis).sum(axis=0)


def cut_along(array, dim, count):
    lengths = array.shape
    tiles = array.reshape(*lengths[:dim], count, lengths[dim] // count, *lengths[dim + 1 :])
    return jnp.moveaxis(tiles, dim, 0)


def laid_out(tiles, dim):
    tiles = jnp.moveaxis(tiles, 0, dim)
    lengths = tiles.shape
    return tiles.reshape(*lengths[:dim], lengths[dim] * lengths[dim + 1], *lengths[dim + 2 :])


def exchange_in_order(tiles, axes, sequence):
    lengths = [lax.axis_size(a) for a in axes]
    tiles = tiles.reshape(*lengths, *tiles.shape[1:])
    for k in sequence:
        tiles = lax.all_to_all(tiles, axes[k], split_axis=k, concat_axis=k, tiled=True)
    return tiles.reshape(-1, *tiles.shape[len(axes) :])


def exchange_by_chip(array, groups, sequence, split_dim, concat_dim):
    count = lax.axis_size(groups[0]) * lax.axis_size(groups[1])
    tiles = cut_along(array, split_dim, count)
    return laid_out(exchange_in_order(tiles, groups, sequence), concat_dim)


def one_exchange(array, axis, axes, splits, concats):
    sizes = [lax.axis_size(a) for a in axes]
    tiles = cut_along(array, splits[0], sizes[0])
    tiles = jnp.moveaxis(cut_along(tiles, splits[1] + 1, sizes[1]), 0, 1)
    inside = tiles.shape[2:]
    tiles = tiles.reshape(-1, *inside)
    tiles = lax.all_to_all(tiles, axis, split_axis=0, concat_axis=0, tiled=True)
    tiles = laid_out(tiles.reshape(*sizes, *inside), concats[0] + 1)
    return laid_out(tiles, concats[1])


def on_device(residuals, owners):
    layer_dev, tok_dev, features = residuals.shape
    groups = lax.axis_size(DP)
    sections = lax.axis_size("section")
    centered = residuals - jnp.mean(residuals, axis=2, keepdims=True)
    partial_value = jnp.sum(centered * centered, axis=(1, 2))
    energy = over_copies(partial_value, DP)
    layer_scale = 1.0 / jnp.sqrt(energy / (tok_dev * groups * features) + 1.0)
    normed = (centered * layer_scale[:, None, None]).astype(jnp.bfloat16).transpose(1, 0, 2)
    spread_rows = exchange_by_chip(normed, (("dp_0", "dp_1"), "dp_2"), (1, 0), 2, 0)
    token_total = spread_rows.shape[0]
    narrow = spread_rows.shape[2]
    blocks_all = owners.shape[0]
    block_len = token_total // blocks_all
    inverse = (
        jnp.zeros((blocks_all,), jnp.int32).at[owners].set(jnp.arange(blocks_all, dtype=jnp.int32))
    )
    ordered = spread_rows.reshape(blocks_all, block_len, layer_dev, narrow)[inverse]
    ordered = ordered.reshape(sections, groups, block_len, layer_dev, narrow)
    received = one_exchange(ordered, DP_SECTION, (DP, "section"), (1, 0), (4, 3))
    return received.reshape(block_len, layer_dev * sections, narrow * groups)


def solution(mesh):
    split = Mesh(
        mesh.devices.reshape(mesh.shape["section"], 4, 4, 2), ("section", "dp_0", "dp_1", "dp_2")
    )
    in_specs = (P("section", DP, None), P())
    out_specs = P(SECTION_DP, None, None)
    return jax.shard_map(
        on_device, mesh=split, in_specs=in_specs, out_specs=out_specs, check_vma=False
    )
```

profile of v0, /device:TPU:1, one launch (start us, length us, event | category | flops | bytes accessed | tf_op | source)
XLA Modules:
  0.0 105.3 jit_solution(16557633780490092673)
XLA Ops:
  0.0 0.0 copy-start
  0.0 1.9 %reduce_sum.27 = f32[4,32]{1,0:T(4,128)S(1)} reduce(f32[4,32,4096]{2,1,0:T(8,128)} %param.2, f32[]{:T(128)} %constant.2.clone.1), dimensions={2}, to_apply=%region_0.0 | reduce | flops 524160 | bytes 2097668 | tf_op jit(solution)/shard_map/reduce_sum | solution.py:62
  1.9 0.3 copy-done
  2.2 0.4 multiply_reduce_fusion
  2.7 17.2 %all_to_all.21 = f32[32,1,4]{2,1,0:T(1,128)S(1)} all-to-all(f32[32,1,4]{2,1,0:T(1,128)S(1)} %broadcast_in_dim.11), channel_id=1, replica_groups=mesh['section'=8,'dp_0'=4,'dp_1'=4,'dp_2'=2] {'dp_0','dp_1','dp_2'}, dimensions={0} | all-to-all | bytes 1024 | tf_op jit(solution)/shard_map/all_to_all | solution.py:14
  19.8 0.1 reduce_sum.29
  19.9 0.3 multiply_convert_fusion
  20.2 0.2 copy.57
  20.5 0.4 copy.46
  20.9 4.8 %all_to_all.22 = bf16[16,2,32,4,128]{4,2,0,3,1:T(8,128)(2,1)S(1)} all-to-all(bf16[16,2,32,4,128]{4,2,0,3,1:T(8,128)(2,1)S(1)} %copy.46), channel_id=1, replica_groups=mesh['section'=8,'dp_0'=4,'dp_1'=4,'dp_2'=2] {'dp_2'}, dimensions={1} | all-to-all | bytes 2097152 | tf_op jit(solution)/shard_map/all_to_all | solution.py:37
  25.7 0.0 copy-start.1
  25.7 1.1 %copy.47 = bf16[16,2,32,4,128]{4,2,1,3,0:T(8,128)(2,1)} copy(bf16[16,2,32,4,128]{4,2,0,3,1:T(8,128)(2,1)S(1)} %all_to_all.22) | data formatting | bytes 2097152 | tf_op jit(solution)/shard_map/all_to_all | solution.py:37
  26.8 3.7 %all-to-all-start.2 = ((bf16[16,2,32,4,128]{4,2,1,3,0:T(8,128)(2,1)}), bf16[16,2,32,4,128]{4,2,1,3,0:T(8,128)(2,1)S(1)}, u32[]{:S(2)}, u32[]{:S(2)}) async-start(bf16[16,2,32,4,128]{4,2,1,3,0:T(8,128)(2,1)} %copy.47), calls=%async_computation.2 | async-start | bytes 2097152 | tf_op jit(solution)/shard_map/all_to_all | solution.py:37
  30.5 0.0 copy-done.1
  30.5 1.4 %scatter_custom_fusion = s32[256]{0:T(256)S(1)} fusion(s32[256]{0:T(256)S(1)} %compare_select_fusion.1, s32[256]{0:T(256)S(1)} %iota.3, s32[]{:T(128)} %constant.12.clone.1), kind=kCustom, calls=%fused_computation.10 | custom fusion | bytes 1028 | tf_op jit(solution)/shard_map/scatter | solution.py:73
  32.0 21.4 %all-to-all-done.2 = bf16[16,2,32,4,128]{4,2,1,3,0:T(8,128)(2,1)S(1)} async-done(((bf16[16,2,32,4,128]{4,2,1,3,0:T(8,128)(2,1)}), bf16[16,2,32,4,128]{4,2,1,3,0:T(8,128)(2,1)S(1)}, u32[]{:S(2)}, u32[]{:S(2)}) %all-to-all-start.2) | async-done | bytes 1048608 | tf_op jit(solution)/shard_map/all_to_all | solution.py:37
  53.4 0.1 copy.48
  53.4 1.9 %gather_fusion = bf16[256,4,4,128]{3,1,2,0:T(4,128)(2,1)S(1)} fusion(bf16[256,4,4,128]{3,1,0,2:T(4,128)(2,1)S(1)} %bitcast.33, s32[1024]{0:T(1024)S(1)} %pad_clamp_fusion), kind=kCustom, calls=%fused_computation | custom fusion | bytes 2098176 | tf_op jit(solution)/shard_map/gather | solution.py:75
  55.3 0.7 copy.61
  56.0 0.8 copy.50
  56.8 45.8 %all_to_all.23 = bf16[256,1,1,4,4,128]{5,4,3,2,1,0:T(4,128)(2,1)S(1)} all-to-all(bf16[256,1,1,4,4,128]{5,4,3,2,1,0:T(4,128)(2,1)S(1)} %copy.50), channel_id=1, replica_groups=mesh['section'=8,'dp_0'=4,'dp_1'=4,'dp_2'=2] {'dp_0','dp_1','dp_2','sect..., dimensions={0} | all-to-all | bytes 2097152 | tf_op jit(solution)/shard_map/all_to_all | solution.py:53
  102.7 0.3 copy.60
  102.9 0.8 copy.52
  103.8 1.6 %copy.53 = bf16[4,32,4096]{2,1,0:T(8,128)(2,1)} copy(bf16[4,32,4096]{2,0,1:T(4,128)(2,1)S(1)} %bitcast.32) | data formatting | bytes 2097152 | tf_op jit(solution)/shard_map/reshape;reshape | solution.py:78
  (7 shorter events, 0.0 us)
Async XLA Ops:
  0.0 2.2 %copy-start = (f32[4,32,4096]{2,1,0:T(8,128)S(1)}, f32[4,32,4096]{2,1,0:T(8,128)}, u32[]{:S(2)}) copy-start(f32[4,32,4096]{2,1,0:T(8,128)} %param.2) | copy-start | bytes 6291460
  25.7 4.8 %copy-start.1 = (s32[256]{0:T(256)S(1)}, s32[256]{0:T(256)}, u32[]{:S(2)}) copy-start(s32[256]{0:T(256)} %param.3) | copy-start | bytes 3076
  26.8 26.5 %all-to-all-start.2 = ((bf16[16,2,32,4,128]{4,2,1,3,0:T(8,128)(2,1)}), bf16[16,2,32,4,128]{4,2,1,3,0:T(8,128)(2,1)S(1)}, u32[]{:S(2)}, u32[]{:S(2)}) async-start(bf16[16,2,32,4,128]{4,2,1,3,0:T(8,128)(2,1)} %copy.47), calls=%async_computation.2 | async-start | bytes 2097152 | tf_op jit(solution)/shard_map/all_to_all | solution.py:37
where the time goes:
time: 106 us; the launch traced here: 105 us
  blocking collectives  67.8 us (64%)
  waiting for transfers between devices  21.4 us (20%)
  local copies, waits for them, and re-layouts  9.57 us (9%)
  starting transfers between devices  3.66 us (3%)
  other arithmetic  2.76 us (3%)
    all_to_all x1, blocking collectives, one_exchange(): tiles = lax.all_to_all(tiles, axis, split_axis=0, concat_axis=0, tiled=True)  45.8 us
    all_to_all x1, waiting for transfers between devices, exchange_in_order(): lax.all_to_all(tiles, axes[k], split_axis=k, concat_axis=k, tiled=True)  21.4 us
    all_to_all x1, blocking collectives, sent_to_all(): return lax.all_to_all(copies, axis, split_axis=0, concat_axis=0, tiled=True)  17.2 us
    all_to_all x1, blocking collectives, exchange_in_order(): lax.all_to_all(tiles, axes[k], split_axis=k, concat_axis=k, tiled=True)  4.84 us
    all_to_all x1, starting transfers between devices, exchange_in_order(): lax.all_to_all(tiles, axes[k], split_axis=k, concat_axis=k, tiled=True)  3.66 us
  transfers between devices with their start and end apart: 1, of which 1 were waited for; matrix products, arithmetic and copies ran while one was open for 1% of the time, Pallas kernels for 0%

commit v1 on v0

v1 whole, which is shorter than its diff:
```python
import jax
import jax.numpy as jnp
from jax import lax
from jax.experimental import pallas as pl
from jax.experimental.pallas import tpu as pltpu
from jax.sharding import Mesh
from jax.sharding import PartitionSpec as P

AXES = ("y", "zh", "zl", "x", "c")
MESH = pl.DeviceIdType.MESH
F32 = jnp.float32
BF16 = jnp.bfloat16
LANES = 128


def device(y, z, x, c):
    return {"y": y, "zh": lax.div(z, 4), "zl": lax.rem(z, 4), "x": x, "c": c}


def whole(ref, count, sem):
    part = ref.at[pl.ds(0, count)]
    return pltpu.make_async_copy(part, part, sem)


def kernel(
    inverse, x_hbm, out, x_in, rows, energy, plane, plane_sum, line,
    split_a, split_b, mixed_a, mixed_b, sorted_a, sorted_b, got_a, got_b,
    in_sem, y_sem, plane_send, plane_recv, line_send, line_recv,
    one_send, one_recv, two_send, two_recv,
):
    layers, tokens, features = x_in.shape
    y, x, c = lax.axis_index("y"), lax.axis_index("x"), lax.axis_index("c")
    zl = lax.axis_index("zl")
    z = lax.axis_index("zh") * 4 + zl
    column = (zl * 4 + x) * 2 + c
    me = (y * 8 + z) * 8 + x * 2 + c
    split, mixed = (split_a, split_b), (mixed_a, mixed_b)
    ordered, got = (sorted_a, sorted_b), (got_a, got_b)

    loads = [
        pltpu.make_async_copy(x_hbm.at[i], x_in.at[i], in_sem.at[i]) for i in range(layers)
    ]
    for load in loads:
        load.start()

    barrier = pltpu.get_barrier_semaphore()
    for step in (4, 3, 5, 2, 6, 1, 7):
        pl.semaphore_signal(
            barrier, inc=1, device_id=device(y, lax.rem(z + step, 8), x, c), device_id_type=MESH
        )
    for step in (2, 1, 3):
        pl.semaphore_signal(
            barrier, inc=1, device_id=device(lax.rem(y + step, 4), z, x, c), device_id_type=MESH
        )

    def near(i):
        return device(y, z, lax.rem(x + lax.div(i, 2), 4), lax.rem(c + lax.rem(i, 2), 2))

    for step in range(1, 8):
        pl.semaphore_signal(barrier, inc=1, device_id=near(step), device_id_type=MESH)

    energy[...] = jnp.zeros_like(energy)
    for layer in range(layers):
        loads[layer].wait()

        def octet(q, total, layer=layer):
            block = x_in[layer, pl.ds(pl.multiple_of(q * 8, 8), 8), :]
            centered = block - jnp.mean(block, axis=1, keepdims=True)
            for j in range(features // LANES):
                piece = centered[:, j * LANES : (j + 1) * LANES]
                total = total + piece * piece
                rows[j, q, pl.ds(layer, 8, stride=4), :] = piece
            return total

        total = lax.fori_loop(0, tokens // 8, octet, jnp.zeros((8, LANES), F32))
        summed = jnp.sum(total, axis=0, keepdims=True)
        energy[layer : layer + 1, :] = summed
        energy[layer + 4 : layer + 5, :] = summed

    slot = x * 2 + c
    plane[slot] = energy[...]
    pl.semaphore_wait(barrier, 17)

    def send_plane(i, _):
        pltpu.make_async_remote_copy(
            energy, plane.at[slot], plane_send, plane_recv, device_id=near(i), device_id_type=MESH
        ).start()
        return 0

    lax.fori_loop(1, 8, send_plane, 0)
    whole(plane, 7, plane_recv).wait()
    partial = plane[0]
    for i in range(1, 8):
        partial = partial + plane[i]
    plane_sum[...] = partial
    line[zl] = partial
    base = lax.div(z, 4) * 4
    for step in (3, 2, 1):
        pltpu.make_async_remote_copy(
            plane_sum, line.at[zl], line_send, line_recv,
            device_id=device(y, base + lax.rem(zl + step, 4), x, c), device_id_type=MESH,
        ).start()
    for step in (2, 1, 3):
        pl.semaphore_signal(
            y_sem, inc=1, device_id=device(lax.rem(y + step, 4), z, x, c), device_id_type=MESH
        )
    whole(line, 3, line_recv).wait()
    sums = (line[0] + line[1]) + (line[2] + line[3])
    sums = jnp.sum(sums, axis=1, keepdims=True)
    scale = 1.0 / jnp.sqrt(sums / (tokens * 32 * features) + 1.0)
    scale = jnp.broadcast_to(scale, (8, LANES))

    for h in range(2):

        def pack(j, _, h=h):
            for q in range(4):
                for k in range(2):
                    piece = rows[j, q, pl.ds(16 * k + 8 * h, 8), :] * scale
                    split[h][j, 2 * q + k] = piece.astype(BF16)
            return 0

        lax.fori_loop(0, 32, pack, 0)
        mixed[h][pl.ds(pl.multiple_of(column * 8, 8), 8)] = split[h][column]
        for near_by in (2, 1, 3, 0):

            def send_one(i, _, h=h, near_by=near_by):
                dx = lax.div(i, 2)
                tx, tc = lax.rem(x + dx, 4), lax.rem(c + lax.rem(i, 2), 2)
                if near_by == 2:
                    tz = lax.rem(z + 2 + 4 * lax.rem(dx + h, 2), 8)
                else:
                    tz = lax.rem(z + (0, 1, 2, 7)[near_by], 8)
                target = (lax.rem(zl + near_by, 4) * 4 + tx) * 2 + tc
                pltpu.make_async_remote_copy(
                    split[h].at[target],
                    mixed[h].at[pl.ds(pl.multiple_of(column * 8, 8), 8)],
                    one_send.at[h], one_recv.at[h],
                    device_id=device(y, tz, tx, tc), device_id_type=MESH,
                ).start()
                return 0

            lax.fori_loop(1 if near_by == 0 else 0, 8, send_one, 0)

    pl.semaphore_wait(y_sem, 3)
    for h in range(2):
        whole(mixed[h], 248, one_recv.at[h]).wait()

        def order(o, _, h=h):
            ordered[h][o] = mixed[h][inverse[o]]
            return 0

        lax.fori_loop(0, 256, order, 0, unroll=8)
        got[h][me] = ordered[h][me]

        def send_two(i, _, h=h):
            ty = lax.rem(y + lax.rem(lax.div(i, 8), 4), 4)
            tz = lax.rem(z + lax.rem(i, 8), 8)
            tx = lax.rem(x + lax.rem(lax.div(i, 32), 4), 4)
            tc = lax.rem(c + lax.div(i, 128), 2)
            target = (ty * 8 + tz) * 8 + tx * 2 + tc
            pltpu.make_async_remote_copy(
                ordered[h].at[target], got[h].at[me], two_send.at[h], two_recv.at[h],
                device_id=device(ty, tz, tx, tc), device_id_type=MESH,
            ).start()
            return 0

        lax.fori_loop(1, 256, send_two, 0)

    block = inverse[me]
    from_z, from_x = lax.div(block, 64), lax.rem(lax.div(block, 16), 4)
    low = lax.broadcasted_iota(jnp.int32, (8, LANES), 0) < 4
    for h in range(2):
        whole(got[h], 255, two_recv.at[h]).wait()

        def place(j, _, h=h):
            away = lax.rem(lax.div(j, 8) - from_z + 4, 4)
            odd = lax.rem(lax.rem(lax.div(j, 2), 4) - from_x + 4 + h, 2)
            move = jnp.where(
                away == 0, 0, jnp.where(away == 1, 1, jnp.where(away == 3, 7, 2 + 4 * odd))
            )
            half = lax.div(lax.rem(from_z + move, 8), 4)
            at = pl.ds(pl.multiple_of(j * LANES, LANES), LANES)
            for k in range(4):
                first = got[h][k * 64 + half * 32 + j].astype(F32)
                second = got[h][k * 64 + (1 - half) * 32 + j].astype(F32)
                upper = jnp.where(low, first, pltpu.roll(second, 4, 0))
                lower = jnp.where(low, pltpu.roll(first, 4, 0), second)
                out[2 * h, pl.ds(8 * k, 8), at] = upper.astype(BF16)
                out[2 * h + 1, pl.ds(8 * k, 8), at] = lower.astype(BF16)
            return 0

        lax.fori_loop(0, 32, place, 0)

    whole(plane, 7, plane_send).wait()
    whole(line, 3, line_send).wait()
    for h in range(2):
        whole(mixed[h], 248, one_send.at[h]).wait()
        whole(got[h], 255, two_send.at[h]).wait()


def on_device(residuals, owners):
    layers, tokens, features = residuals.shape
    blocks = owners.shape[0]
    numbers = jnp.arange(blocks, dtype=jnp.int32)
    inverse = jnp.sum(
        jnp.where(owners[None, :] == numbers[:, None], numbers[None, :], 0), axis=1
    )
    dma = pltpu.SemaphoreType.DMA
    vmem = pltpu.VMEM
    return pl.pallas_call(
        kernel,
        out_shape=jax.ShapeDtypeStruct((4, 8 * layers, features), BF16),
        in_specs=[
            pl.BlockSpec(memory_space=pltpu.SMEM),
            pl.BlockSpec(memory_space=pl.ANY),
        ],
        out_specs=pl.BlockSpec(memory_space=pltpu.VMEM),
        scratch_shapes=[
            vmem((layers, tokens, features), F32),
            vmem((32, 4, 32, LANES), F32),
            vmem((8, LANES), F32),
            vmem((8, 8, LANES), F32),
            vmem((8, LANES), F32),
            vmem((4, 8, LANES), F32),
            vmem((32, 8, 8, LANES), BF16),
            vmem((32, 8, 8, LANES), BF16),
            vmem((blocks, 8, LANES), BF16),
            vmem((blocks, 8, LANES), BF16),
            vmem((blocks, 8, LANES), BF16),
            vmem((blocks, 8, LANES), BF16),
            vmem((blocks, 8, LANES), BF16),
            vmem((blocks, 8, LANES), BF16),
            dma((layers,)),
            pltpu.SemaphoreType.REGULAR,
            dma, dma, dma, dma,
            dma((2,)), dma((2,)), dma((2,)), dma((2,)),
        ],
        compiler_params=pltpu.CompilerParams(collective_id=0, has_side_effects=True),
    )(inverse, residuals)


def solution(mesh):
    split = Mesh(mesh.devices.reshape(4, 2, 4, 4, 2), AXES)
    return jax.shard_map(
        on_device,
        mesh=split,
        in_specs=(P(("y", "zh"), ("zl", "x", "c"), None), P()),
        out_specs=P(AXES, None, None),
        check_vma=False,
    )
```

time: 106 us -> 62.7 us (0.59)
  blocking collectives: 67.8 us -> 0 us
  Pallas kernels: 0 us -> 58.9 us
  waiting for transfers between devices: 21.4 us -> 0 us
  local copies, waits for them, and re-layouts: 9.57 us -> 2.29 us
  starting transfers between devices: 3.66 us -> 0 us
  other arithmetic: 2.76 us -> 1.36 us
    all_to_all x3 -> x0, blocking collectives: 67.8 us -> none  [the longest x1 45.8 us: one_exchange(): tiles = lax.all_to_all(tiles, axis, split_axis=0, concat_axis=0, tiled=True)]
    pallas_call x0 -> x1, Pallas kernels: none -> 58.9 us  [on_device(): pl.pallas_call(kernel, out_shape=jax.ShapeDtypeStruct((4, 8 * layers, fea...]
    all_to_all x1 -> x0, waiting for transfers between devices: 21.4 us -> none  [exchange_in_order(): lax.all_to_all(tiles, axes[k], split_axis=k, concat_axis=k, tiled=True)]
    all_to_all x1 -> x0, starting transfers between devices: 3.66 us -> none  [exchange_in_order(): lax.all_to_all(tiles, axes[k], split_axis=k, concat_axis=k, tiled=True)]
    another operation x3 -> x0, local copies, waits for them, and re-layouts: 3.04 us -> none  [the longest x1 1.55 us: on_device(): return received.reshape(block_len, layer_dev * sections, narrow * groups)]
    gather x1 -> x0, local copies, waits for them, and re-layouts: 1.88 us -> none  [on_device(): spread_rows.reshape(blocks_all, block_len, layer_dev, narrow)[inverse]]
    unnamed x5 -> x1, local copies, waits for them, and re-layouts: 0.53 us -> 2.29 us
    all_to_all x3 -> x0, local copies, waits for them, and re-layouts: 1.48 us -> none  [the longest x2 1.21 us: exchange_in_order(): lax.all_to_all(tiles, axes[k], split_axis=k, concat_axis=k, tiled=True)]
  transfers between devices with their start and end apart: 1 -> 0, of which waited for: 1 -> 0; matrix products, arithmetic and copies ran while one was open for 1% -> 0% of each run, Pallas kernels for 0% -> 0%
where the time goes in v1:
time: 62.7 us; the launch traced here: 62.5 us
  Pallas kernels  58.9 us (94%)
  local copies, waits for them, and re-layouts  2.29 us (4%)
  other arithmetic  1.36 us (2%)
    pallas_call x1, Pallas kernels, on_device(): pl.pallas_call(kernel, out_shape=jax.ShapeDtypeStruct((4, 8 * layers, fea...  58.9 us
    unnamed x1, local copies, waits for them, and re-layouts  2.29 us
    reduce_sum x1, other arithmetic, on_device(): jnp.sum(jnp.where(owners[None, :] == numbers[:, None], numbers[None, :],...  1.36 us

profile of v1, /device:TPU:1, one launch (start us, length us, event | category | flops | bytes accessed | tf_op | source)
XLA Modules:
  0.0 62.5 jit_solution(8944830398218652715)
XLA Ops:
  0.0 1.4 %select_reduce_fusion.inverse = s32[256]{0:T(256)} fusion(s32[256]{0:T(256)} %param.3), kind=kLoop, calls=%fused_computation | loop fusion | flops 196352 | bytes 2048 | tf_op jit(solution)/shard_map/reduce_sum | solution.py:205
  1.4 58.9 %shard_map.28 = bf16[4,32,4096]{2,1,0:T(8,128)(2,1)} custom-call(s32[256]{0:T(256)} %select_reduce_fusion.inverse, f32[4,32,4096]{2,1,0:T(8,128)} %x_hbm.1), custom_call_target="tpu_custom_call" | custom-call | tf_op jit(solution)/shard_map/pallas_call | solution.py:210
  60.2 2.3 %copy.4 = bf16[4,32,4096]{2,1,0:T(8,128)(2,1)} copy(bf16[4,32,4096]{2,1,0:T(8,128)(2,1)} %shard_map.28) | data formatting | bytes 2097152

commit v2 on v1

v2 whole, which is shorter than its diff:
```python
import jax
import jax.numpy as jnp
from jax import lax
from jax.experimental import pallas as pl
from jax.experimental.pallas import tpu as pltpu
from jax.sharding import PartitionSpec as P

MESH = pl.DeviceIdType.MESH
F32 = jnp.float32
BF16 = jnp.bfloat16
LANES = 128


def device(number):
    return {"section": lax.div(number, 32), "dp": lax.rem(number, 32)}


def whole(ref, count, sem):
    part = ref.at[pl.ds(0, count)]
    return pltpu.make_async_copy(part, part, sem)


def kernel(
    owners_hbm, x_hbm, out, owners, inverse, found, x_in, sums, means, rows, energy, plane,
    plane_sum, line, split_a, split_b, mixed_a, mixed_b, sorted_a, sorted_b, got_a, got_b,
    in_sem, own_sem, y_sem, plane_send, plane_recv, line_send, line_recv,
    one_send, one_recv, two_send, two_recv,
):
    layers, tokens, features = x_in.shape
    octets, slices = tokens // 8, features // LANES
    section, column = lax.axis_index("section"), lax.axis_index("dp")
    y, zh = lax.div(section, 2), lax.rem(section, 2)
    zl, slot = lax.div(column, 8), lax.rem(column, 8)
    z = zh * 4 + zl
    x = lax.div(slot, 2)
    me = section * 32 + column
    split, mixed = (split_a, split_b), (mixed_a, mixed_b)
    ordered, got = (sorted_a, sorted_b), (got_a, got_b)

    loads = [
        pltpu.make_async_copy(x_hbm.at[i], x_in.at[i], in_sem.at[i]) for i in range(layers)
    ]
    for load in loads:
        load.start()
    fetch = pltpu.make_async_copy(owners_hbm, owners, own_sem.at[0])
    fetch.start()

    def signal(sem, target):
        pl.semaphore_signal(sem, inc=1, device_id=device(target), device_id_type=MESH)

    barrier = pltpu.get_barrier_semaphore()
    for step in (3, 5, 2, 6, 1, 7):
        signal(barrier, y * 64 + lax.rem(z + step, 8) * 8 + slot)
    for step in (2, 1, 3):
        signal(barrier, lax.rem(y + step, 4) * 64 + z * 8 + slot)
    for step in range(1, 8):
        signal(barrier, y * 64 + z * 8 + lax.rem(slot + step, 8))

    for layer in range(layers):
        loads[layer].wait()

        def add_up(q, _, layer=layer):
            at = pl.ds(pl.multiple_of(q * 8, 8), 8)
            parts = [x_in[layer, at, j * LANES : (j + 1) * LANES] for j in range(slices)]
            while len(parts) > 1:
                parts = [a + b for a, b in zip(parts[::2], parts[1::2])]
            sums[layer * octets + q] = parts[0]
            return 0

        lax.fori_loop(0, octets, add_up, 0)
    mean = jnp.sum(sums[...], axis=2, keepdims=True) / features
    means[...] = jnp.broadcast_to(mean, means.shape)

    for layer in range(layers):

        def squares(q, totals, layer=layer):
            at = pl.ds(pl.multiple_of(q * 8, 8), 8)
            mean = means[layer * octets + q]
            totals = list(totals)
            for j in range(slices):
                piece = x_in[layer, at, j * LANES : (j + 1) * LANES] - mean
                totals[j % 4] = totals[j % 4] + piece * piece
            return tuple(totals)

        zero = jnp.zeros((8, LANES), F32)
        totals = lax.fori_loop(0, octets, squares, (zero,) * 4)
        total = (totals[0] + totals[1]) + (totals[2] + totals[3])
        summed = jnp.sum(total, axis=0, keepdims=True)
        energy[layer : layer + 1, :] = summed
        energy[layer + 4 : layer + 5, :] = summed

    plane[slot] = energy[...]
    pl.semaphore_wait(barrier, 16)
    for step in range(1, 8):
        pltpu.make_async_remote_copy(
            energy, plane.at[slot], plane_send, plane_recv,
            device_id=device(y * 64 + z * 8 + lax.rem(slot + step, 8)), device_id_type=MESH,
        ).start()

    for layer in range(layers):

        def arrange(q, _, layer=layer):
            at = pl.ds(pl.multiple_of(q * 8, 8), 8)
            mean = means[layer * octets + q]
            for j in range(slices):
                piece = x_in[layer, at, j * LANES : (j + 1) * LANES] - mean
                rows[j, q, pl.ds(layer, 8, stride=4), :] = piece
            return 0

        lax.fori_loop(0, octets, arrange, 0)

    whole(plane, 7, plane_recv).wait()
    partial = plane[0]
    for i in range(1, 8):
        partial = partial + plane[i]
    plane_sum[...] = partial
    line[zl] = partial
    for step in (3, 2, 1):
        pltpu.make_async_remote_copy(
            plane_sum, line.at[zl], line_send, line_recv,
            device_id=device(y * 64 + zh * 32 + lax.rem(zl + step, 4) * 8 + slot), device_id_type=MESH,
        ).start()
    for step in (2, 1, 3):
        signal(y_sem, lax.rem(y + step, 4) * 64 + z * 8 + slot)
    whole(line, 3, line_recv).wait()
    total = (line[0] + line[1]) + (line[2] + line[3])
    total = jnp.sum(total, axis=1, keepdims=True)
    scale = 1.0 / jnp.sqrt(total / (tokens * 32 * features) + 1.0)
    scale = jnp.broadcast_to(scale, (8, LANES))

    my_blocks = pl.ds(pl.multiple_of(column * 8, 8), 8)
    for h in range(2):
        for away in (2, 1, 3, 0):
            first = lax.rem(zl + away, 4) * 8

            def pack(i, _, h=h, first=first):
                for q in range(octets):
                    for k in range(2):
                        piece = rows[first + i, q, pl.ds(16 * k + 8 * h, 8), :] * scale
                        split[h][first + i, 2 * q + k] = piece.astype(BF16)
                return 0

            lax.fori_loop(0, 8, pack, 0)
            for i in range(1 if away == 0 else 0, 8):
                there = lax.rem(slot + i, 8)
                if away == 2:
                    odd = lax.rem(lax.div(there, 2) + x + h, 2)
                    tz = lax.rem(z + 2 + 4 * odd, 8)
                else:
                    tz = lax.rem(z + (0, 1, 2, 7)[away], 8)
                pltpu.make_async_remote_copy(
                    split[h].at[first + there], mixed[h].at[my_blocks],
                    one_send.at[h], one_recv.at[h],
                    device_id=device(y * 64 + tz * 8 + there), device_id_type=MESH,
                ).start()
        mixed[h][my_blocks] = split[h][column]

    fetch.wait()
    numbers = (
        lax.broadcasted_iota(jnp.int32, (8, LANES), 0) * LANES
        + lax.broadcasted_iota(jnp.int32, (8, LANES), 1)
    )

    def invert(b, known):
        return jnp.where(numbers == owners[b], b, known)

    found[...] = lax.fori_loop(0, 256, invert, jnp.zeros((8, LANES), jnp.int32), unroll=8)
    pl.semaphore_wait(y_sem, 3)
    table = pltpu.make_async_copy(found, inverse, own_sem.at[1])
    table.start()
    table.wait()

    for h in range(2):
        whole(mixed[h], 248, one_recv.at[h]).wait()
        for top in range(2):

            def order(o, _, h=h, top=top):
                ordered[h][top * LANES + o] = mixed[h][inverse[top, o]]
                return 0

            lax.fori_loop(0, LANES, order, 0, unroll=8)

        def send_two(i, _, h=h):
            target = lax.rem(me + i, 256)
            pltpu.make_async_remote_copy(
                ordered[h].at[target], got[h].at[me], two_send.at[h], two_recv.at[h],
                device_id=device(target), device_id_type=MESH,
            ).start()
            return 0

        lax.fori_loop(1, 256, send_two, 0)
        got[h][me] = ordered[h][me]

    block = inverse[lax.div(me, LANES), lax.rem(me, LANES)]
    from_z, from_x = lax.div(block, 64), lax.rem(lax.div(block, 2 * 8), 4)
    low = lax.broadcasted_iota(jnp.int32, (8, LANES), 0) < 4
    for h in range(2):
        whole(got[h], 255, two_recv.at[h]).wait()

        def place(j, _, h=h):
            away = lax.rem(lax.div(j, 8) - from_z + 4, 4)
            odd = lax.rem(lax.rem(lax.div(j, 2), 4) - from_x + 4 + h, 2)
            move = jnp.where(
                away == 0, 0, jnp.where(away == 1, 1, jnp.where(away == 3, 7, 2 + 4 * odd))
            )
            half = lax.div(lax.rem(from_z + move, 8), 4)
            at = pl.ds(pl.multiple_of(j * LANES, LANES), LANES)
            for k in range(4):
                first = got[h][k * 64 + half * 32 + j].astype(F32)
                second = got[h][k * 64 + (1 - half) * 32 + j].astype(F32)
                upper = jnp.where(low, first, pltpu.roll(second, 4, 0))
                lower = jnp.where(low, pltpu.roll(first, 4, 0), second)
                out[2 * h, pl.ds(8 * k, 8), at] = upper.astype(BF16)
                out[2 * h + 1, pl.ds(8 * k, 8), at] = lower.astype(BF16)
            return 0

        lax.fori_loop(0, slices, place, 0)

    whole(plane, 7, plane_send).wait()
    whole(line, 3, line_send).wait()
    for h in range(2):
        whole(mixed[h], 248, one_send.at[h]).wait()
        whole(got[h], 255, two_send.at[h]).wait()


def on_device(residuals, owners):
    layers, tokens, features = residuals.shape
    blocks = owners.shape[0]
    dma, vmem = pltpu.SemaphoreType.DMA, pltpu.VMEM
    tile = vmem((8, LANES), F32)
    pieces = vmem((blocks, 8, LANES), BF16)
    octets = layers * tokens // 8
    return pl.pallas_call(
        kernel,
        out_shape=jax.ShapeDtypeStruct((4, 8 * layers, features), BF16),
        in_specs=[pl.BlockSpec(memory_space=pltpu.HBM)] * 2,
        out_specs=pl.BlockSpec(memory_space=pltpu.VMEM),
        scratch_shapes=[
            pltpu.SMEM((blocks,), jnp.int32),
            pltpu.SMEM((8, LANES), jnp.int32),
            vmem((8, LANES), jnp.int32),
            vmem((layers, tokens, features), F32),
            vmem((octets, 8, LANES), F32),
            vmem((octets, 8, LANES), F32),
            vmem((features // LANES, tokens // 8, 32, LANES), F32),
            tile,
            vmem((8, 8, LANES), F32),
            tile,
            vmem((4, 8, LANES), F32),
            vmem((32, 8, 8, LANES), BF16),
            vmem((32, 8, 8, LANES), BF16),
            pieces, pieces, pieces, pieces, pieces, pieces,
            dma((layers,)),
            dma((2,)),
            pltpu.SemaphoreType.REGULAR,
            dma, dma, dma, dma,
            dma((2,)), dma((2,)), dma((2,)), dma((2,)),
        ],
        compiler_params=pltpu.CompilerParams(
            collective_id=0, has_side_effects=True, vmem_limit_bytes=16 * 2**20
        ),
    )(*(pltpu.with_memory_space_constraint(a, pltpu.HBM) for a in (owners, residuals)))


def solution(mesh):
    return jax.shard_map(
        on_device,
        mesh=mesh,
        in_specs=(P("section", "dp", None), P()),
        out_specs=P(("section", "dp"), None, None),
        check_vma=False,
    )
```

time: 62.7 us -> 56.1 us (0.89)
  Pallas kernels: 58.9 us -> 55.1 us
  other arithmetic: 1.36 us -> 0 us
  local copies, waits for them, and re-layouts: 2.29 us -> 0.97 us
    pallas_call x1, Pallas kernels: 58.9 us -> 55.1 us  [on_device(): pl.pallas_call(kernel, out_shape=jax.ShapeDtypeStruct((4, 8 * layers, fea...]
    reduce_sum x1 -> x0, other arithmetic: 1.36 us -> none  [on_device(): jnp.sum(jnp.where(owners[None, :] == numbers[:, None], numbers[None, :],...]
    unnamed x1, local copies, waits for them, and re-layouts: 2.29 us -> 0.97 us
where the time goes in v2:
time: 56.1 us; the launch traced here: 56 us
  Pallas kernels  55.1 us (98%)
  local copies, waits for them, and re-layouts  0.97 us (2%)
    pallas_call x1, Pallas kernels, on_device(): pl.pallas_call(kernel, out_shape=jax.ShapeDtypeStruct((4, 8 * layers, fea...  55.1 us

profile of v2, /device:TPU:1, one launch (start us, length us, event | category | flops | bytes accessed | tf_op | source)
XLA Modules:
  0.0 56.0 jit_solution(8825317803717119047)
XLA Ops:
  0.0 55.1 %shard_map.28 = bf16[4,32,4096]{2,1,0:T(8,128)(2,1)S(1)} custom-call(s32[256]{0:T(256)} %owners_hbm.1, f32[4,32,4096]{2,1,0:T(8,128)} %x_hbm.1), custom_call_target="tpu_custom_call" | custom-call | tf_op jit(solution)/shard_map/pallas_call | solution.py:233
  55.1 1.0 %copy.4 = bf16[4,32,4096]{2,1,0:T(8,128)(2,1)} copy(bf16[4,32,4096]{2,1,0:T(8,128)(2,1)S(1)} %shard_map.28) | data formatting | bytes 2097152

commit v3 on v2

--- a/solution.py
+++ b/solution.py
@@ -9,6 +9,9 @@
 F32 = jnp.float32
 BF16 = jnp.bfloat16
 LANES = 128
+EARLY = ((0, 0), (0, 1), (1, 0), (3, 0))
+FIRST = 2
+LATE = 248 - 16 * len(EARLY)
 
 
 def device(number):
@@ -22,8 +25,9 @@
 
 def kernel(
     owners_hbm, x_hbm, out, owners, inverse, found, x_in, sums, means, rows, energy, plane,
-    plane_sum, line, split_a, split_b, mixed_a, mixed_b, sorted_a, sorted_b, got_a, got_b,
+    plane_sum, line, scales, ahead, early, split_a, split_b, mixed_a, mixed_b, sorted_a, sorted_b, got_a, got_b,
     in_sem, own_sem, y_sem, plane_send, plane_recv, line_send, line_recv,
+    scale_send, scale_recv, early_send, early_recv,
     one_send, one_recv, two_send, two_recv,
 ):
     layers, tokens, features = x_in.shape
@@ -32,7 +36,7 @@
     y, zh = lax.div(section, 2), lax.rem(section, 2)
     zl, slot = lax.div(column, 8), lax.rem(column, 8)
     z = zh * 4 + zl
-    x = lax.div(slot, 2)
+    x, c = lax.div(slot, 2), lax.rem(slot, 2)
     me = section * 32 + column
     split, mixed = (split_a, split_b), (mixed_a, mixed_b)
     ordered, got = (sorted_a, sorted_b), (got_a, got_b)
@@ -53,6 +57,8 @@
         signal(barrier, y * 64 + lax.rem(z + step, 8) * 8 + slot)
     for step in (2, 1, 3):
         signal(barrier, lax.rem(y + step, 4) * 64 + z * 8 + slot)
+    for step in (1, 7):
+        signal(barrier, y * 64 + lax.rem(z + step, 8) * 8 + x * 2 + 1 - c)
     for step in range(1, 8):
         signal(barrier, y * 64 + z * 8 + lax.rem(slot + step, 8))
 
@@ -90,24 +96,45 @@
         energy[layer + 4 : layer + 5, :] = summed
 
     plane[slot] = energy[...]
-    pl.semaphore_wait(barrier, 16)
+    pl.semaphore_wait(barrier, 18)
     for step in range(1, 8):
         pltpu.make_async_remote_copy(
             energy, plane.at[slot], plane_send, plane_recv,
             device_id=device(y * 64 + z * 8 + lax.rem(slot + step, 8)), device_id_type=MESH,
         ).start()
 
-    for layer in range(layers):
-
-        def arrange(q, _, layer=layer):
-            at = pl.ds(pl.multiple_of(q * 8, 8), 8)
-            mean = means[layer * octets + q]
-            for j in range(slices):
-                piece = x_in[layer, at, j * LANES : (j + 1) * LANES] - mean
-                rows[j, q, pl.ds(layer, 8, stride=4), :] = piece
-            return 0
-
-        lax.fori_loop(0, octets, arrange, 0)
+    def arrange(j, into):
+        lanes = pl.ds(pl.multiple_of(j * LANES, LANES), LANES)
+        for layer in range(layers):
+            for q in range(octets):
+                piece = x_in[layer, q * 8 : q * 8 + 8, lanes] - means[layer * octets + q]
+                into[q, pl.ds(layer, 8, stride=4), :] = piece
+
+    def slot_at(dx, dc):
+        return lax.rem(x + dx, 4) * 2 + lax.rem(c + dc, 2)
+
+    def send_early(steps):
+        for k in steps:
+            there = slot_at(*EARLY[k])
+            for i, (away, move) in enumerate(((1, 1), (3, 7))):
+                source = rows.at[lax.rem(zl + away, 4) * 8 + there]
+                pltpu.make_async_remote_copy(
+                    ahead.at[2 * k + i] if k < FIRST else source, early.at[2 * k + i],
+                    early_send, early_recv,
+                    device_id=device(y * 64 + lax.rem(z + move, 8) * 8 + there),
+                    device_id_type=MESH,
+                ).start()
+
+    for k in range(FIRST):
+        for i, away in enumerate((1, 3)):
+            arrange(lax.rem(zl + away, 4) * 8 + slot_at(*EARLY[k]), ahead.at[2 * k + i])
+    send_early(range(FIRST))
+
+    def arrange_all(j, _):
+        arrange(j, rows.at[j])
+        return 0
+
+    lax.fori_loop(0, slices, arrange_all, 0)
 
     whole(plane, 7, plane_recv).wait()
     partial = plane[0]
@@ -120,16 +147,31 @@
             plane_sum, line.at[zl], line_send, line_recv,
             device_id=device(y * 64 + zh * 32 + lax.rem(zl + step, 4) * 8 + slot), device_id_type=MESH,
         ).start()
+    send_early(range(FIRST, len(EARLY)))
     for step in (2, 1, 3):
         signal(y_sem, lax.rem(y + step, 4) * 64 + z * 8 + slot)
+    fetch.wait()
+    numbers = (
+        lax.broadcasted_iota(jnp.int32, (8, LANES), 0) * LANES
+        + lax.broadcasted_iota(jnp.int32, (8, LANES), 1)
+    )
+
+    def invert(b, known):
+        return jnp.where(numbers == owners[b], b, known)
+
+    found[...] = lax.fori_loop(0, 256, invert, jnp.zeros((8, LANES), jnp.int32), unroll=8)
+    table = pltpu.make_async_copy(found, inverse, own_sem.at[1])
+    table.start()
     whole(line, 3, line_recv).wait()
     total = (line[0] + line[1]) + (line[2] + line[3])
     total = jnp.sum(total, axis=1, keepdims=True)
     scale = 1.0 / jnp.sqrt(total / (tokens * 32 * features) + 1.0)
     scale = jnp.broadcast_to(scale, (8, LANES))
+    scales[2] = scale
 
     my_blocks = pl.ds(pl.multiple_of(column * 8, 8), 8)
     for h in range(2):
+        if h == 1: whole(mixed[0], LATE, one_send.at[0]).wait()
         for away in (2, 1, 3, 0):
             first = lax.rem(zl + away, 4) * 8
 
@@ -141,11 +183,19 @@
                 return 0
 
             lax.fori_loop(0, 8, pack, 0)
-            for i in range(1 if away == 0 else 0, 8):
-                there = lax.rem(slot + i, 8)
+            if h == 0 and away == 2:
+                for i, move in enumerate((1, 7)):
+                    pltpu.make_async_remote_copy(
+                        scales.at[2], scales.at[i], scale_send, scale_recv,
+                        device_id=device(y * 64 + lax.rem(z + move, 8) * 8 + slot),
+                        device_id_type=MESH,
+                    ).start()
+            for dx, dc in ((2, 0), (2, 1), (1, 0), (3, 0), (1, 1), (3, 1), (0, 1), (0, 0)):
+                if (away == 0 and dx + dc == 0) or (away in (1, 3) and (dx, dc) in EARLY):
+                    continue
+                there = slot_at(dx, dc)
                 if away == 2:
-                    odd = lax.rem(lax.div(there, 2) + x + h, 2)
-                    tz = lax.rem(z + 2 + 4 * odd, 8)
+                    tz = lax.rem(z + 2 + 4 * ((dx + h) % 2), 8)
                 else:
                     tz = lax.rem(z + (0, 1, 2, 7)[away], 8)
                 pltpu.make_async_remote_copy(
@@ -155,23 +205,20 @@
                 ).start()
         mixed[h][my_blocks] = split[h][column]
 
-    fetch.wait()
-    numbers = (
-        lax.broadcasted_iota(jnp.int32, (8, LANES), 0) * LANES
-        + lax.broadcasted_iota(jnp.int32, (8, LANES), 1)
-    )
-
-    def invert(b, known):
-        return jnp.where(numbers == owners[b], b, known)
-
-    found[...] = lax.fori_loop(0, 256, invert, jnp.zeros((8, LANES), jnp.int32), unroll=8)
+    table.wait()
     pl.semaphore_wait(y_sem, 3)
-    table = pltpu.make_async_copy(found, inverse, own_sem.at[1])
-    table.start()
-    table.wait()
-
+    whole(scales, 2, scale_recv).wait()
+    whole(early, 2 * len(EARLY), early_recv).wait()
     for h in range(2):
-        whole(mixed[h], 248, one_recv.at[h]).wait()
+        for k, (dx, dc) in enumerate(EARLY):
+            for i, away in enumerate((3, 1)):
+                source = lax.rem(zl + away, 4) * 8 + slot_at((4 - dx) % 4, dc)
+                for q in range(octets):
+                    for part in range(2):
+                        low = 16 * part + 8 * h
+                        piece = early[2 * k + i, q, low : low + 8, :] * scales[i]
+                        mixed[h][source * 8 + 2 * q + part] = piece.astype(BF16)
+        whole(mixed[h], LATE, one_recv.at[h]).wait()
         for top in range(2):
 
             def order(o, _, h=h, top=top):
@@ -197,29 +244,33 @@
     for h in range(2):
         whole(got[h], 255, two_recv.at[h]).wait()
 
-        def place(j, _, h=h):
-            away = lax.rem(lax.div(j, 8) - from_z + 4, 4)
-            odd = lax.rem(lax.rem(lax.div(j, 2), 4) - from_x + 4 + h, 2)
-            move = jnp.where(
-                away == 0, 0, jnp.where(away == 1, 1, jnp.where(away == 3, 7, 2 + 4 * odd))
-            )
-            half = lax.div(lax.rem(from_z + move, 8), 4)
-            at = pl.ds(pl.multiple_of(j * LANES, LANES), LANES)
-            for k in range(4):
-                first = got[h][k * 64 + half * 32 + j].astype(F32)
-                second = got[h][k * 64 + (1 - half) * 32 + j].astype(F32)
-                upper = jnp.where(low, first, pltpu.roll(second, 4, 0))
-                lower = jnp.where(low, pltpu.roll(first, 4, 0), second)
-                out[2 * h, pl.ds(8 * k, 8), at] = upper.astype(BF16)
-                out[2 * h + 1, pl.ds(8 * k, 8), at] = lower.astype(BF16)
+        def place(there, _, h=h):
+            away = lax.rem(there - from_z + 4, 4)
+            for odd in range(2):
+                far = lax.rem(odd + from_x + h, 2)
+                move = jnp.where(away == 3, 7, jnp.where(away == 2, 2 + 4 * far, away))
+                half = lax.div(lax.rem(from_z + move, 8), 4)
+                for k in range(4):
+                    near_at = k * 64 + half * 32 + there * 8
+                    far_at = k * 64 + (1 - half) * 32 + there * 8
+                    for i in (2 * odd, 2 * odd + 1, 2 * odd + 4, 2 * odd + 5):
+                        at = pl.ds(pl.multiple_of((there * 8 + i) * LANES, LANES), LANES)
+                        first = got[h][near_at + i].astype(F32)
+                        second = got[h][far_at + i].astype(F32)
+                        upper = jnp.where(low, first, pltpu.roll(second, 4, 0))
+                        lower = jnp.where(low, pltpu.roll(first, 4, 0), second)
+                        out[2 * h, pl.ds(8 * k, 8), at] = upper.astype(BF16)
+                        out[2 * h + 1, pl.ds(8 * k, 8), at] = lower.astype(BF16)
             return 0
 
-        lax.fori_loop(0, slices, place, 0)
+        lax.fori_loop(0, 4, place, 0)
 
     whole(plane, 7, plane_send).wait()
     whole(line, 3, line_send).wait()
+    whole(scales, 2, scale_send).wait()
+    whole(early, 2 * len(EARLY), early_send).wait()
     for h in range(2):
-        whole(mixed[h], 248, one_send.at[h]).wait()
+        if h == 1: whole(mixed[h], LATE, one_send.at[h]).wait()
         whole(got[h], 255, two_send.at[h]).wait()
 
 
@@ -247,13 +298,16 @@
             vmem((8, 8, LANES), F32),
             tile,
             vmem((4, 8, LANES), F32),
+            vmem((3, 8, LANES), F32),
+            vmem((2 * FIRST, tokens // 8, 32, LANES), F32),
+            vmem((2 * len(EARLY), tokens // 8, 32, LANES), F32),
             vmem((32, 8, 8, LANES), BF16),
             vmem((32, 8, 8, LANES), BF16),
             pieces, pieces, pieces, pieces, pieces, pieces,
             dma((layers,)),
             dma((2,)),
             pltpu.SemaphoreType.REGULAR,
-            dma, dma, dma, dma,
+            dma, dma, dma, dma, dma, dma, dma, dma,
             dma((2,)), dma((2,)), dma((2,)), dma((2,)),
         ],
         compiler_params=pltpu.CompilerParams(

time: 56.1 us -> 54.3 us (0.968)
  Pallas kernels: 55.1 us -> 53.2 us
    pallas_call x1, Pallas kernels: 55.1 us -> 53.2 us  [on_device(): pl.pallas_call(kernel, out_shape=jax.ShapeDtypeStruct((4, 8 * layers, fea...]
where the time goes in v3:
time: 54.3 us; the launch traced here: 54.2 us
  Pallas kernels  53.2 us (98%)
  local copies, waits for them, and re-layouts  0.97 us (2%)
    pallas_call x1, Pallas kernels, on_device(): pl.pallas_call(kernel, out_shape=jax.ShapeDtypeStruct((4, 8 * layers, fea...  53.2 us

profile of v3, /device:TPU:1, one launch (start us, length us, event | category | flops | bytes accessed | tf_op | source)
XLA Modules:
  0.0 54.2 jit_solution(16575700553658212117)
XLA Ops:
  0.0 53.2 %shard_map.28 = bf16[4,32,4096]{2,1,0:T(8,128)(2,1)S(1)} custom-call(s32[256]{0:T(256)} %owners_hbm.1, f32[4,32,4096]{2,1,0:T(8,128)} %x_hbm.1), custom_call_target="tpu_custom_call" | custom-call | tf_op jit(solution)/shard_map/pallas_call | solution.py:284
  53.2 1.0 %copy.4 = bf16[4,32,4096]{2,1,0:T(8,128)(2,1)} copy(bf16[4,32,4096]{2,1,0:T(8,128)(2,1)S(1)} %shard_map.28) | data formatting | bytes 2097152

commit v4 on v3

--- a/solution.py
+++ b/solution.py
@@ -9,8 +9,10 @@
 F32 = jnp.float32
 BF16 = jnp.bfloat16
 LANES = 128
-EARLY = ((0, 0), (0, 1), (1, 0), (3, 0))
+EARLY = ((0, 0), (0, 1), (1, 0), (3, 1))
 FIRST = 2
+FRONT = 1
+RATE = 2
 LATE = 248 - 16 * len(EARLY)
 
 
@@ -227,15 +229,35 @@
 
             lax.fori_loop(0, LANES, order, 0, unroll=8)
 
-        def send_two(i, _, h=h):
-            target = lax.rem(me + i, 256)
-            pltpu.make_async_remote_copy(
-                ordered[h].at[target], got[h].at[me], two_send.at[h], two_recv.at[h],
-                device_id=device(target), device_id_type=MESH,
-            ).start()
+        def send_two(tz, offset, h=h):
+            across = lax.rem(y * 8 + slot + offset, 32)
+            ty, there = lax.div(across, 8), lax.rem(across, 8)
+            target = ty * 64 + tz * 8 + there
+
+            @pl.when(target != me)
+            def _():
+                to = {"section": ty * 2 + lax.div(tz, 4), "dp": lax.rem(tz, 4) * 8 + there}
+                pltpu.make_async_remote_copy(
+                    ordered[h].at[target], got[h].at[me], two_send.at[h], two_recv.at[h],
+                    device_id=to, device_id_type=MESH,
+                ).start()
+
+        def send_mixed(i, _):
+            for k in range(RATE):
+                n = i * RATE + k
+                send_two(lax.rem(n, FRONT), lax.div(n, FRONT))
+            for tz in range(FRONT, 8):
+                send_two(tz, i)
             return 0
 
-        lax.fori_loop(1, 256, send_two, 0)
+        def send_rest(i, _):
+            for tz in range(FRONT, 8):
+                send_two(tz, i)
+            return 0
+
+        steps = FRONT * 32 // RATE
+        lax.fori_loop(0, steps, send_mixed, 0)
+        lax.fori_loop(steps, 32, send_rest, 0)
         got[h][me] = ordered[h][me]
 
     block = inverse[lax.div(me, LANES), lax.rem(me, LANES)]

time: 54.3 us -> 53.1 us (0.978)
  the two profiles are of different devices: /device:TPU:1 before, /device:TPU:39 now
where the time goes in v4:
time: 53.1 us; the launch traced here: 53 us
  Pallas kernels  52.1 us (98%)
  local copies, waits for them, and re-layouts  0.97 us (2%)
    pallas_call x1, Pallas kernels, on_device(): pl.pallas_call(kernel, out_shape=jax.ShapeDtypeStruct((4, 8 * layers, fea...  52.1 us

profile of v4, /device:TPU:39, one launch (start us, length us, event | category | flops | bytes accessed | tf_op | source)
XLA Modules:
  0.0 53.0 jit_solution(13139842210317383872)
XLA Ops:
  0.0 52.1 %shard_map.28 = bf16[4,32,4096]{2,1,0:T(8,128)(2,1)S(1)} custom-call(s32[256]{0:T(256)} %owners_hbm.1, f32[4,32,4096]{2,1,0:T(8,128)} %x_hbm.1), custom_call_target="tpu_custom_call" | custom-call | tf_op jit(solution)/shard_map/pallas_call | solution.py:306
  52.1 1.0 %copy.4 = bf16[4,32,4096]{2,1,0:T(8,128)(2,1)} copy(bf16[4,32,4096]{2,1,0:T(8,128)(2,1)S(1)} %shard_map.28) | data formatting | bytes 2097152

commit v5 on v4

--- a/solution.py
+++ b/solution.py
@@ -55,14 +55,14 @@
         pl.semaphore_signal(sem, inc=1, device_id=device(target), device_id_type=MESH)
 
     barrier = pltpu.get_barrier_semaphore()
+    for step in (4, 5, 3, 2, 6, 7, 1):
+        signal(barrier, y * 64 + z * 8 + lax.rem(slot + step, 8))
     for step in (3, 5, 2, 6, 1, 7):
         signal(barrier, y * 64 + lax.rem(z + step, 8) * 8 + slot)
     for step in (2, 1, 3):
         signal(barrier, lax.rem(y + step, 4) * 64 + z * 8 + slot)
     for step in (1, 7):
         signal(barrier, y * 64 + lax.rem(z + step, 8) * 8 + x * 2 + 1 - c)
-    for step in range(1, 8):
-        signal(barrier, y * 64 + z * 8 + lax.rem(slot + step, 8))
 
     for layer in range(layers):
         loads[layer].wait()
@@ -95,11 +95,10 @@
         total = (totals[0] + totals[1]) + (totals[2] + totals[3])
         summed = jnp.sum(total, axis=0, keepdims=True)
         energy[layer : layer + 1, :] = summed
-        energy[layer + 4 : layer + 5, :] = summed
 
     plane[slot] = energy[...]
     pl.semaphore_wait(barrier, 18)
-    for step in range(1, 8):
+    for step in (4, 5, 3, 2, 6, 7, 1):
         pltpu.make_async_remote_copy(
             energy, plane.at[slot], plane_send, plane_recv,
             device_id=device(y * 64 + z * 8 + lax.rem(slot + step, 8)), device_id_type=MESH,
@@ -166,7 +165,7 @@
     table.start()
     whole(line, 3, line_recv).wait()
     total = (line[0] + line[1]) + (line[2] + line[3])
-    total = jnp.sum(total, axis=1, keepdims=True)
+    total = jnp.sum(jnp.concatenate([total, total], axis=0), axis=1, keepdims=True)
     scale = 1.0 / jnp.sqrt(total / (tokens * 32 * features) + 1.0)
     scale = jnp.broadcast_to(scale, (8, LANES))
     scales[2] = scale
@@ -316,10 +315,10 @@
             vmem((octets, 8, LANES), F32),
             vmem((octets, 8, LANES), F32),
             vmem((features // LANES, tokens // 8, 32, LANES), F32),
-            tile,
-            vmem((8, 8, LANES), F32),
-            tile,
-            vmem((4, 8, LANES), F32),
+            vmem((layers, LANES), F32),
+            vmem((8, layers, LANES), F32),
+            vmem((layers, LANES), F32),
+            vmem((4, layers, LANES), F32),
             vmem((3, 8, LANES), F32),
             vmem((2 * FIRST, tokens // 8, 32, LANES), F32),
             vmem((2 * len(EARLY), tokens // 8, 32, LANES), F32),

time: 53.1 us -> 53 us (level)
  no operation moved by 1% of the time
where the time goes in v5:
time: 53 us; the launch traced here: 52.9 us
  Pallas kernels  51.9 us (98%)
  local copies, waits for them, and re-layouts  0.97 us (2%)
    pallas_call x1, Pallas kernels, on_device(): pl.pallas_call(kernel, out_shape=jax.ShapeDtypeStruct((4, 8 * layers, fea...  51.9 us

profile of v5, /device:TPU:39, one launch (start us, length us, event | category | flops | bytes accessed | tf_op | source)
XLA Modules:
  0.0 52.9 jit_solution(12638159487421972757)
XLA Ops:
  0.0 51.9 %shard_map.28 = bf16[4,32,4096]{2,1,0:T(8,128)(2,1)S(1)} custom-call(s32[256]{0:T(256)} %owners_hbm.1, f32[4,32,4096]{2,1,0:T(8,128)} %x_hbm.1), custom_call_target="tpu_custom_call" | custom-call | tf_op jit(solution)/shard_map/pallas_call | solution.py:305
  51.9 1.0 %copy.4 = bf16[4,32,4096]{2,1,0:T(8,128)(2,1)} copy(bf16[4,32,4096]{2,1,0:T(8,128)(2,1)S(1)} %shard_map.28) | data formatting | bytes 2097152

commit v6 on v5

--- a/solution.py
+++ b/solution.py
@@ -295,6 +295,17 @@
         whole(got[h], 255, two_send.at[h]).wait()
 
 
+def write_out(placed, out, sem):
+    copies = [
+        pltpu.make_async_copy(placed.at[i // 2, pl.ds(16 * (i % 2), 16)], out.at[i // 2, pl.ds(16 * (i % 2), 16)], sem.at[i])
+        for i in range(8)
+    ]
+    for copy in copies:
+        copy.start()
+    for copy in copies:
+        copy.wait()
+
+
 def on_device(residuals, owners):
     layers, tokens, features = residuals.shape
     blocks = owners.shape[0]
@@ -302,7 +313,7 @@
     tile = vmem((8, LANES), F32)
     pieces = vmem((blocks, 8, LANES), BF16)
     octets = layers * tokens // 8
-    return pl.pallas_call(
+    placed = pl.pallas_call(
         kernel,
         out_shape=jax.ShapeDtypeStruct((4, 8 * layers, features), BF16),
         in_specs=[pl.BlockSpec(memory_space=pltpu.HBM)] * 2,
@@ -335,6 +346,14 @@
             collective_id=0, has_side_effects=True, vmem_limit_bytes=16 * 2**20
         ),
     )(*(pltpu.with_memory_space_constraint(a, pltpu.HBM) for a in (owners, residuals)))
+    return pl.pallas_call(
+        write_out,
+        out_shape=jax.ShapeDtypeStruct(placed.shape, placed.dtype),
+        in_specs=[pl.BlockSpec(memory_space=pltpu.VMEM)],
+        out_specs=pl.BlockSpec(memory_space=pltpu.HBM),
+        scratch_shapes=[dma((8,))],
+        compiler_params=pltpu.CompilerParams(vmem_limit_bytes=16 * 2**20),
+    )(placed)
 
 
 def solution(mesh):

time: 53 us -> 53 us (level)
  Pallas kernels: 51.9 us -> 52.9 us
  local copies, waits for them, and re-layouts: 0.97 us -> 0 us
    pallas_call x0 -> x1, Pallas kernels: none -> 1.03 us  [on_device(): pl.pallas_call(write_out, out_shape=jax.ShapeDtypeStruct(placed.shape, pl...]
    unnamed x1 -> x0, local copies, waits for them, and re-layouts: 0.97 us -> none
where the time goes in v6:
time: 53 us; the launch traced here: 52.9 us
  Pallas kernels  52.9 us (100%)
    pallas_call x1, Pallas kernels, on_device(): pl.pallas_call(kernel, out_shape=jax.ShapeDtypeStruct((4, 8 * layers, fea...  51.9 us

profile of v6, /device:TPU:39, one launch (start us, length us, event | category | flops | bytes accessed | tf_op | source)
XLA Modules:
  0.0 52.9 jit_solution(9219906989415764135)
XLA Ops:
  0.0 51.9 %shard_map.28.placed = bf16[4,32,4096]{2,1,0:T(8,128)(2,1)S(1)} custom-call(s32[256]{0:T(256)} %owners_hbm.1, f32[4,32,4096]{2,1,0:T(8,128)} %x_hbm.1), custom_call_target="tpu_custom_call" | custom-call | tf_op jit(solution)/shard_map/pallas_call | solution.py:316
  51.9 1.0 %shard_map.29 = bf16[4,32,4096]{2,1,0:T(8,128)(2,1)} custom-call(bf16[4,32,4096]{2,1,0:T(8,128)(2,1)S(1)} %shard_map.28.placed), custom_call_target="tpu_custom_call" | custom-call | tf_op jit(solution)/shard_map/pallas_call | solution.py:349
